TPU v7x, 512 devices: a whole 4x8x8 slice. The times are simulated.
512 devices in a mesh: out: 16 (over x_hi, y), in: 32 (over x_lo, z, core).
Axes of the slice: x: 4 (x_hi: 2, x_lo: 2; x = x_hi * 2 + x_lo), y: 8, z: 8, core: 2. Of those that a mesh axis runs over, the one named last changes fastest.
Arguments:
- gradients: bfloat16 [1024, 28672], P('out', 'in'), may hold values from -6 to 6
- activations: bfloat16 [1024, 8192], P('in', 'out'), may hold values from -6 to 6
- out_basis: bfloat16 [28672, 14336], P('in', 'out'), may hold values from -0.03125 to 0.03125
- in_basis: bfloat16 [8192, 8192], P('out', 'in'), may hold values from -0.0625 to 0.0625
- eigen_table: float32 [14336, 8192], P('out', 'in'), may hold values from 0.1 to 2
Outputs:
- updated_table: float32 [14336, 8192], P('out', 'in')
All inputs are finite; a program needn't handle non-finite values.
Results may differ from a plain program's by a relative error of at most 0.002.
Values may be sent and summed in bfloat16 or wider, within the bound.
No kernel may reach another device: no remote copies, remote signals or barrier semaphores. Data moves between devices by JAX's collectives and lax.ppermute only.
A program may use at most 64 MiB of HBM per device.

v0:
```python
import jax
import jax.numpy as jnp
from jax import lax
from jax.sharding import PartitionSpec as P

LEN = 128


def from_everyone(value, axis):
    size = lax.axis_size(axis)
    return lax.all_to_all(
        jnp.broadcast_to(value[None], (size, *value.shape)), axis, 0, 0, tiled=True
    )


def in_order(pieces, dim):
    dims = list(pieces.shape[1:])
    dims[dim] *= pieces.shape[0]
    return jnp.moveaxis(pieces, 0, dim).reshape(dims)


def collect(value, axis, dim):
    pieces = from_everyone(value, axis)
    return in_order(pieces, dim)


def local(gradients, activations, out_basis, in_basis, eigen_table):
    partial_grad = jnp.dot(
        lax.all_gather(gradients, "out", axis=0, tiled=True),
        out_basis,
        preferred_element_type=jnp.float32,
    )
    partial_act = jnp.dot(
        collect(activations, "in", 0), in_basis, preferred_element_type=jnp.float32
    )
    rotated_grad = lax.psum(partial_grad, "in").astype(jnp.bfloat16)
    rotated_act = lax.psum(partial_act, "out").astype(jnp.bfloat16)
    token_count = rotated_grad.shape[0]
    seq_count = token_count // LEN
    grad_blocks = rotated_grad.reshape(seq_count, LEN, rotated_grad.shape[1])
    act_blocks = rotated_act.reshape(seq_count, LEN, rotated_act.shape[1])
    corr = jnp.einsum("stn,stm->snm", grad_blocks, act_blocks, preferred_element_type=jnp.float32)
    return eigen_table + jnp.sum(corr * corr, axis=0) / token_count


def solution(mesh):
    return jax.shard_map(
        local,
        mesh=mesh,
        in_specs=(P("out", "in"), P("in", "out"), P("in", "out"), P("out", "in"), P("out", "in")),
        out_specs=P("out", "in"),
        check_vma=False,
    )
```

profile of v0, /device:TPU:2, one launch (start us, length us, event | category | flops | bytes accessed | tf_op | source)
XLA Modules:
  0.0 284.9 jit_solution(765318451840276056)
XLA Ops:
  6.5 0.0 copy-start
  6.5 0.0 copy-start.2
  6.5 0.0 all-gather.2.cloned.1.call-start
  6.5 0.7 all-gather.2.cloned.1.call-update
  7.3 0.9 broadcast_in_dim.2
  8.1 39.1 %all_to_all.5 = bf16[32,32,512]{2,1,0:T(8,128)(2,1)S(1)} all-to-all(bf16[32,32,512]{2,1,0:T(8,128)(2,1)S(1)} %broadcast_in_dim.2), channel_id=1, replica_groups=mesh['out'=16,'in'=32] {'in'}, dimensions={0} | all-to-all | bytes 2097152 | tf_op jit(solution)/shard_map/all_to_all | solution.py:11
  47.3 0.0 copy-done.2
  47.3 0.4 fusion.1
  47.7 93.1 %all-reduce.3 = bf16[1024,256]{1,0:T(8,128)(2,1)} all-reduce(f32[1024,256]{1,0:T(8,128)S(1)} %fusion.1), channel_id=1, replica_groups=mesh['out'=16,'in'=32] {'out'}, use_global_device_ids=true, to_apply=%region_1.0 | all-reduce | flops 262144 | bytes 1572864 | tf_op jit(solution)/shard_map/psum | solution.py:37
  140.8 0.0 all-gather.2.cloned.1.call-done
  140.8 0.0 copy-done
  140.8 5.5 %fusion = f32[1024,896]{1,0:T(8,128)} fusion(bf16[1024,896]{1,0:T(8,128)(2,1)} %all-gather.2.cloned.1.call-done, bf16[896,896]{1,0:T(8,128)(2,1)S(1)} %copy-done), kind=kOutput, calls=%fused_computation.2 | convolution fusion | flops 1644167168 | bytes 7110656 | tf_op jit(solution)/shard_map/dot_general | solution.py:28
  146.4 128.3 %all-reduce.2 = bf16[1024,896]{1,0:T(8,128)(2,1)S(1)} all-reduce(f32[1024,896]{1,0:T(8,128)} %fusion), channel_id=1, replica_groups=mesh['out'=16,'in'=32] {'in'}, use_global_device_ids=true, to_apply=%region_0.0 | all-reduce | flops 917504 | bytes 5505024 | tf_op jit(solution)/shard_map/psum | solution.py:36
  274.7 0.0 copy-start.1
  274.7 2.3 multiply_reduce_fusion
  277.0 0.0 copy-done.1
  277.0 1.0 multiply_add_fusion
Async XLA Ops:
  6.5 134.3 %copy-start = (bf16[896,896]{1,0:T(8,128)(2,1)S(1)}, bf16[896,896]{1,0:T(8,128)(2,1)}, u32[]{:S(2)}) copy-start(bf16[896,896]{1,0:T(8,128)(2,1)} %param.7) | copy-start | bytes 4816900
  6.5 40.7 %copy-start.2 = (bf16[512,256]{1,0:T(8,128)(2,1)S(1)}, bf16[512,256]{1,0:T(8,128)(2,1)}, u32[]{:S(2)}) copy-start(bf16[512,256]{1,0:T(8,128)(2,1)} %param.8) | copy-start | bytes 786436
  6.5 134.3 %all-gather.2.cloned.1.call-start = ((), (), s32[]{:S(2)}) async-start(), calls=%async_computation.1 | async-start | bytes 1949696 | tf_op jit(solution)/shard_map/all_gather | solution.py:29
  274.7 2.4 copy-start.1
Sparse Core Ops, SparseCore 0:
  10.5 96.6 all-gather.1
where the time goes:
time: 285 us
  blocking collectives  261 us (92%)
  between operations  13.4 us (5%)
  matrix products  8.31 us (3%)
    psum x1, blocking collectives, local(): rotated_grad = lax.psum(partial_grad, 'in').astype(jnp.bfloat16)  128 us
    psum x1, blocking collectives, local(): rotated_act = lax.psum(partial_act, 'out').astype(jnp.bfloat16)  93.1 us
    all_to_all x1, blocking collectives, from_everyone(): lax.all_to_all(jnp.broadcast_to(value[None], (size, *value.shape)), axis,...  39.1 us
  transfers between devices with their start and end apart: 1, of which 0 were waited for; matrix products, arithmetic and copies ran while one was open for 0% of the time, Pallas kernels for 0%

commit v1 on v0

v1 whole, which is shorter than its diff:
```python
import jax
import jax.numpy as jnp
from jax import lax
from jax.sharding import Mesh, PartitionSpec as P

LEN = 128
OUT = ("xh", "y")
CHIPS = ("xl", "z")


def swap(value):
    return lax.ppermute(value, "c", [(0, 1), (1, 0)])


def exchange(pieces, axes):
    return lax.all_to_all(pieces, axes, 0, 0, tiled=True)


def spread(value, axes):
    size = lax.axis_size(axes)
    return exchange(jnp.broadcast_to(value[None], (size, *value.shape)), axes)


def reduce_rows(partial, axes):
    size = lax.axis_size(axes)
    rows, columns = partial.shape
    pieces = partial.astype(jnp.bfloat16).reshape(size, rows // size, columns)
    received = exchange(pieces, axes)
    return jnp.sum(received.astype(jnp.float32), axis=0).astype(jnp.bfloat16)


def local(gradients, activations, out_basis, in_basis, eigen_table):
    f32 = jnp.float32
    core = lax.axis_index("c")
    rows, features = gradients.shape
    half = rows // 2
    mine = lax.dynamic_slice_in_dim(gradients, core * half, half, 0)
    theirs = lax.dynamic_slice_in_dim(gradients, (1 - core) * half, half, 0)
    wide = jnp.concatenate([mine, swap(theirs)], axis=1)
    basis_other = swap(out_basis)

    wide = spread(wide, OUT)
    wide = wide.reshape(-1, wide.shape[2])
    partial_grad = jnp.dot(wide[:, :features], out_basis, preferred_element_type=f32)
    partial_grad += jnp.dot(wide[:, features:], basis_other, preferred_element_type=f32)
    grad_rows = reduce_rows(partial_grad, CHIPS)
    grads = spread(grad_rows, CHIPS)
    grads = jnp.stack([grads, swap(grads)], axis=1)

    acts = spread(activations, CHIPS)
    acts = acts.reshape(-1, acts.shape[2])
    acts = jnp.concatenate([acts, swap(acts)], axis=0)
    partial_act = jnp.dot(acts, in_basis, preferred_element_type=f32)
    act_rows = reduce_rows(partial_act, OUT)
    acts = spread(act_rows, OUT).reshape(2, -1, half, act_rows.shape[1])
    acts = jnp.stack([acts[0], acts[1]], axis=1)

    token_count = rows * lax.axis_size(OUT)
    grad_blocks = grads.reshape(token_count // LEN, LEN, grads.shape[-1])
    act_blocks = acts.reshape(token_count // LEN, LEN, acts.shape[-1])
    corr = jnp.einsum("stn,stm->snm", grad_blocks, act_blocks, preferred_element_type=f32)
    return eigen_table + jnp.sum(corr * corr, axis=0) / token_count


def solution(mesh):
    chips = Mesh(mesh.devices.reshape(2, 8, 2, 8, 2), ("xh", "y", "xl", "z", "c"))
    out_axes, in_axes = ("xh", "y"), ("xl", "z", "c")
    by_out, by_in = P(out_axes, in_axes), P(in_axes, out_axes)
    return jax.shard_map(
        local,
        mesh=chips,
        in_specs=(by_out, by_in, by_in, by_out, by_out),
        out_specs=by_out,
        check_vma=False,
    )
```

time: 285 us -> 193 us (0.68)
  the two profiles are of different devices: /device:TPU:2 before, /device:TPU:8 now
where the time goes in v1:
time: 193 us; the launch traced here: 192 us
  waiting for transfers between devices  119 us (62%)
  starting transfers between devices  57.6 us (30%)
  matrix products  8.6 us (4%)
  local copies, waits for them, and re-layouts  5.09 us (3%)
    all_to_all x6, waiting for transfers between devices, exchange(): return lax.all_to_all(pieces, axes, 0, 0, tiled=True)  116 us
    all_to_all x6, starting transfers between devices, exchange(): return lax.all_to_all(pieces, axes, 0, 0, tiled=True)  49.9 us
    ppermute x4, starting transfers between devices, swap(): return lax.ppermute(value, 'c', [(0, 1), (1, 0)])  7.66 us
    broadcast_in_dim x4, local copies, waits for them, and re-layouts, spread(): return exchange(jnp.broadcast_to(value[None], (size, *value.shape)), axes)  4.13 us
  transfers between devices with their start and end apart: 10, of which 8 were waited for; matrix products, arithmetic and copies ran while one was open for 4% of the time, Pallas kernels for 0%

profile of v1, /device:TPU:8, one launch (start us, length us, event | category | flops | bytes accessed | tf_op | source)
XLA Modules:
  0.0 191.9 jit_solution(3957500431817356763)
XLA Ops:
  0.0 0.0 copy-start
  0.0 0.9 constant_dynamic-slice_fusion.1
  0.9 1.9 %collective-permute-start = (bf16[32,896]{1,0:T(8,128)(2,1)S(1)}, bf16[32,896]{1,0:T(8,128)(2,1)S(1)}, u32[]{:S(2)}, u32[]{:S(2)}) collective-permute-start(bf16[32,896]{1,0:T(8,128)(2,1)S(1)} %get-tuple-element.8), channel_id=1, source_target_pairs={{0,1},{1,0},{2,3},{3,2},{4,5},{5,4},{6,7},{7,6},{8,9},{9,8},{10,11... | collective-permute-start | bytes 172040 | tf_op jit(solution)/shard_map/ppermute | solution.py:12
  2.8 1.2 collective-permute-done
  4.1 1.4 broadcast_in_dim.8
  5.5 0.0 copy-start.2
  5.5 10.2 %all-to-all-start = ((bf16[16,32,1792]{2,1,0:T(8,128)(2,1)}), bf16[16,32,1792]{2,1,0:T(8,128)(2,1)S(1)}, u32[]{:S(2)}, u32[]{:S(2)}) async-start(bf16[16,32,1792]{2,1,0:T(8,128)(2,1)} %broadcast_in_dim.8), calls=%async_computation | async-start | bytes 3670016 | tf_op jit(solution)/shard_map/all_to_all | solution.py:16
  15.7 1.9 collective-permute-start.1
  17.6 43.2 %all-to-all-done = bf16[16,32,1792]{2,1,0:T(8,128)(2,1)S(1)} async-done(((bf16[16,32,1792]{2,1,0:T(8,128)(2,1)}), bf16[16,32,1792]{2,1,0:T(8,128)(2,1)S(1)}, u32[]{:S(2)}, u32[]{:S(2)}) %all-to-all-start) | async-done | bytes 1835040 | tf_op jit(solution)/shard_map/all_to_all | solution.py:16
  60.8 0.0 copy-done.2
  60.8 0.9 broadcast_in_dim.10
  61.6 10.4 %all-to-all-start.3 = ((bf16[16,32,512]{2,1,0:T(8,128)(2,1)}), bf16[16,32,512]{2,1,0:T(8,128)(2,1)S(1)}, u32[]{:S(2)}, u32[]{:S(2)}) async-start(bf16[16,32,512]{2,1,0:T(8,128)(2,1)} %broadcast_in_dim.10), calls=%async_computation.3 | async-start | bytes 1048576 | tf_op jit(solution)/shard_map/all_to_all | solution.py:16
  72.1 2.6 %fusion.4 = f32[512,896]{1,0:T(8,128)S(1)} fusion(bf16[896,896]{1,0:T(8,128)(2,1)} %param.7, bf16[512,1792]{1,0:T(8,128)(2,1)S(1)} %bitcast.18), kind=kOutput, calls=%fused_computation.8 | convolution fusion | flops 822083584 | bytes 4358144 | tf_op jit(solution)/shard_map/dot_general | solution.py:44
  74.7 0.0 collective-permute-done.1
  74.7 3.6 %add_convert_fusion = bf16[512,896]{1,0:T(8,128)(2,1)} fusion(f32[512,896]{1,0:T(8,128)S(1)} %fusion.4, bf16[896,896]{1,0:T(8,128)(2,1)} %collective-permute-done.1, bf16[512,1792]{1,0:T(8,128)(2,1)S(1)} %bitcast.19), kind=kOutput, calls=%fused_computation.2 | convolution fusion | flops 823001088 | bytes 5275648 | tf_op jit(solution)/shard_map/dot_general | solution.py:45
  78.3 7.1 %all-to-all-done.3 = bf16[16,32,512]{2,1,0:T(8,128)(2,1)S(1)} async-done(((bf16[16,32,512]{2,1,0:T(8,128)(2,1)}), bf16[16,32,512]{2,1,0:T(8,128)(2,1)S(1)}, u32[]{:S(2)}, u32[]{:S(2)}) %all-to-all-start.3) | async-done | bytes 524320 | tf_op jit(solution)/shard_map/all_to_all | solution.py:16
  85.4 4.9 %all-to-all-start.1 = ((bf16[16,32,896]{2,1,0:T(8,128)(2,1)}), bf16[16,32,896]{2,1,0:T(8,128)(2,1)S(1)}, u32[]{:S(2)}, u32[]{:S(2)}) async-start(bf16[16,32,896]{2,1,0:T(8,128)(2,1)} %bitcast.1), calls=%async_computation.1 | async-start | bytes 1835008 | tf_op jit(solution)/shard_map/all_to_all | solution.py:16
  90.3 1.9 %collective-permute-start.3 = (bf16[512,512]{1,0:T(8,128)(2,1)S(1)}, bf16[512,512]{1,0:T(8,128)(2,1)S(1)}, u32[]{:S(2)}, u32[]{:S(2)}) collective-permute-start(bf16[512,512]{1,0:T(8,128)(2,1)S(1)} %bitcast.24), channel_id=1, source_target_pairs={{0,1},{1,0},{2,3},{3,2},{4,5},{5,4},{6,7},{7,6},{8,9},{9,8},{10,11... | collective-permute-start | bytes 1572872 | tf_op jit(solution)/shard_map/ppermute | solution.py:12
  92.3 1.9 collective-permute-done.3
  94.1 0.0 copy-done
  94.1 1.2 convolution_convert_fusion
  95.4 17.2 %all-to-all-done.1 = bf16[16,32,896]{2,1,0:T(8,128)(2,1)S(1)} async-done(((bf16[16,32,896]{2,1,0:T(8,128)(2,1)}), bf16[16,32,896]{2,1,0:T(8,128)(2,1)S(1)}, u32[]{:S(2)}, u32[]{:S(2)}) %all-to-all-start.1) | async-done | bytes 917536 | tf_op jit(solution)/shard_map/all_to_all | solution.py:16
  112.6 10.3 %all-to-all-start.4 = ((bf16[16,64,256]{2,1,0:T(8,128)(2,1)}), bf16[16,64,256]{2,1,0:T(8,128)(2,1)S(1)}, u32[]{:S(2)}, u32[]{:S(2)}) async-start(bf16[16,64,256]{2,1,0:T(8,128)(2,1)} %bitcast.7), calls=%async_computation.4 | async-start | bytes 1048576 | tf_op jit(solution)/shard_map/all_to_all | solution.py:16
  122.9 0.1 reduce_sum.33
  123.1 14.2 %all-to-all-done.4 = bf16[16,64,256]{2,1,0:T(8,128)(2,1)S(1)} async-done(((bf16[16,64,256]{2,1,0:T(8,128)(2,1)}), bf16[16,64,256]{2,1,0:T(8,128)(2,1)S(1)}, u32[]{:S(2)}, u32[]{:S(2)}) %all-to-all-start.4) | async-done | bytes 524320 | tf_op jit(solution)/shard_map/all_to_all | solution.py:16
  137.3 1.0 broadcast_in_dim.9
  138.3 5.8 %all-to-all-start.2 = ((bf16[16,32,896]{2,1,0:T(8,128)(2,1)}), bf16[16,32,896]{2,1,0:T(8,128)(2,1)S(1)}, u32[]{:S(2)}, u32[]{:S(2)}) async-start(bf16[16,32,896]{2,1,0:T(8,128)(2,1)} %broadcast_in_dim.9), calls=%async_computation.2 | async-start | bytes 1835008 | tf_op jit(solution)/shard_map/all_to_all | solution.py:16
  144.1 0.1 reduce_sum.34
  144.2 21.7 %all-to-all-done.2 = bf16[16,32,896]{2,1,0:T(8,128)(2,1)S(1)} async-done(((bf16[16,32,896]{2,1,0:T(8,128)(2,1)}), bf16[16,32,896]{2,1,0:T(8,128)(2,1)S(1)}, u32[]{:S(2)}, u32[]{:S(2)}) %all-to-all-start.2) | async-done | bytes 917536 | tf_op jit(solution)/shard_map/all_to_all | solution.py:16
  165.9 0.8 broadcast_in_dim.11
  166.8 8.2 %all-to-all-start.5 = ((bf16[16,64,256]{2,1,0:T(8,128)(2,1)}), bf16[16,64,256]{2,1,0:T(8,128)(2,1)S(1)}, u32[]{:S(2)}, u32[]{:S(2)}) async-start(bf16[16,64,256]{2,1,0:T(8,128)(2,1)} %broadcast_in_dim.11), calls=%async_computation.5 | async-start | bytes 1048576 | tf_op jit(solution)/shard_map/all_to_all | solution.py:16
  175.0 1.9 collective-permute-start.2
  176.9 12.4 %all-to-all-done.5 = bf16[16,64,256]{2,1,0:T(8,128)(2,1)S(1)} async-done(((bf16[16,64,256]{2,1,0:T(8,128)(2,1)}), bf16[16,64,256]{2,1,0:T(8,128)(2,1)S(1)}, u32[]{:S(2)}, u32[]{:S(2)}) %all-to-all-start.5) | async-done | bytes 524320 | tf_op jit(solution)/shard_map/all_to_all | solution.py:16
  189.4 0.1 pad_maximum_fusion.1
  189.4 0.0 collective-permute-done.2
  189.4 0.2 pad_maximum_fusion
  189.6 0.0 copy-start.1
  189.7 1.2 multiply_reduce_fusion
  190.8 0.0 copy-done.1
  190.8 1.0 multiply_add_fusion
  (2 shorter events, 0.1 us)
Async XLA Ops:
  0.0 94.1 %copy-start = (bf16[512,256]{1,0:T(8,128)(2,1)S(1)}, bf16[512,256]{1,0:T(8,128)(2,1)}, u32[]{:S(2)}) copy-start(bf16[512,256]{1,0:T(8,128)(2,1)} %param.8) | copy-start | bytes 786436
  0.9 3.1 %collective-permute-start = (bf16[32,896]{1,0:T(8,128)(2,1)S(1)}, bf16[32,896]{1,0:T(8,128)(2,1)S(1)}, u32[]{:S(2)}, u32[]{:S(2)}) collective-permute-start(bf16[32,896]{1,0:T(8,128)(2,1)S(1)} %get-tuple-element.8), channel_id=1, source_target_pairs={{0,1},{1,0},{2,3},{3,2},{4,5},{5,4},{6,7},{7,6},{8,9},{9,8},{10,11... | collective-permute-start | bytes 172040 | tf_op jit(solution)/shard_map/ppermute | solution.py:12
  5.5 55.3 %copy-start.2 = (bf16[32,512]{1,0:T(8,128)(2,1)S(1)}, bf16[32,512]{1,0:T(8,128)(2,1)}, u32[]{:S(2)}) copy-start(bf16[32,512]{1,0:T(8,128)(2,1)} %param.6) | copy-start | bytes 98308
  5.5 55.3 %all-to-all-start = ((bf16[16,32,1792]{2,1,0:T(8,128)(2,1)}), bf16[16,32,1792]{2,1,0:T(8,128)(2,1)S(1)}, u32[]{:S(2)}, u32[]{:S(2)}) async-start(bf16[16,32,1792]{2,1,0:T(8,128)(2,1)} %broadcast_in_dim.8), calls=%async_computation | async-start | bytes 3670016 | tf_op jit(solution)/shard_map/all_to_all | solution.py:16
  15.7 59.0 %collective-permute-start.1 = (bf16[896,896]{1,0:T(8,128)(2,1)}, bf16[896,896]{1,0:T(8,128)(2,1)}, u32[]{:S(2)}, u32[]{:S(2)}) collective-permute-start(bf16[896,896]{1,0:T(8,128)(2,1)} %param.7), channel_id=1, source_target_pairs={{0,1},{1,0},{2,3},{3,2},{4,5},{5,4},{6,7},{7,6},{8,9},{9,8},{10,11... | collective-permute-start | bytes 4816904 | tf_op jit(solution)/shard_map/ppermute | solution.py:12
  61.6 23.8 %all-to-all-start.3 = ((bf16[16,32,512]{2,1,0:T(8,128)(2,1)}), bf16[16,32,512]{2,1,0:T(8,128)(2,1)S(1)}, u32[]{:S(2)}, u32[]{:S(2)}) async-start(bf16[16,32,512]{2,1,0:T(8,128)(2,1)} %broadcast_in_dim.10), calls=%async_computation.3 | async-start | bytes 1048576 | tf_op jit(solution)/shard_map/all_to_all | solution.py:16
  85.4 27.2 %all-to-all-start.1 = ((bf16[16,32,896]{2,1,0:T(8,128)(2,1)}), bf16[16,32,896]{2,1,0:T(8,128)(2,1)S(1)}, u32[]{:S(2)}, u32[]{:S(2)}) async-start(bf16[16,32,896]{2,1,0:T(8,128)(2,1)} %bitcast.1), calls=%async_computation.1 | async-start | bytes 1835008 | tf_op jit(solution)/shard_map/all_to_all | solution.py:16
  90.3 3.8 %collective-permute-start.3 = (bf16[512,512]{1,0:T(8,128)(2,1)S(1)}, bf16[512,512]{1,0:T(8,128)(2,1)S(1)}, u32[]{:S(2)}, u32[]{:S(2)}) collective-permute-start(bf16[512,512]{1,0:T(8,128)(2,1)S(1)} %bitcast.24), channel_id=1, source_target_pairs={{0,1},{1,0},{2,3},{3,2},{4,5},{5,4},{6,7},{7,6},{8,9},{9,8},{10,11... | collective-permute-start | bytes 1572872 | tf_op jit(solution)/shard_map/ppermute | solution.py:12
  112.6 24.7 %all-to-all-start.4 = ((bf16[16,64,256]{2,1,0:T(8,128)(2,1)}), bf16[16,64,256]{2,1,0:T(8,128)(2,1)S(1)}, u32[]{:S(2)}, u32[]{:S(2)}) async-start(bf16[16,64,256]{2,1,0:T(8,128)(2,1)} %bitcast.7), calls=%async_computation.4 | async-start | bytes 1048576 | tf_op jit(solution)/shard_map/all_to_all | solution.py:16
  138.3 27.6 %all-to-all-start.2 = ((bf16[16,32,896]{2,1,0:T(8,128)(2,1)}), bf16[16,32,896]{2,1,0:T(8,128)(2,1)S(1)}, u32[]{:S(2)}, u32[]{:S(2)}) async-start(bf16[16,32,896]{2,1,0:T(8,128)(2,1)} %broadcast_in_dim.9), calls=%async_computation.2 | async-start | bytes 1835008 | tf_op jit(solution)/shard_map/all_to_all | solution.py:16
  166.8 22.6 %all-to-all-start.5 = ((bf16[16,64,256]{2,1,0:T(8,128)(2,1)}), bf16[16,64,256]{2,1,0:T(8,128)(2,1)S(1)}, u32[]{:S(2)}, u32[]{:S(2)}) async-start(bf16[16,64,256]{2,1,0:T(8,128)(2,1)} %broadcast_in_dim.11), calls=%async_computation.5 | async-start | bytes 1048576 | tf_op jit(solution)/shard_map/all_to_all | solution.py:16
  175.0 14.4 %collective-permute-start.2 = (bf16[16,32,896]{2,1,0:T(8,128)(2,1)S(1)}, bf16[16,32,896]{2,1,0:T(8,128)(2,1)S(1)}, u32[]{:S(2)}, u32[]{:S(2)}) collective-permute-start(bf16[16,32,896]{2,1,0:T(8,128)(2,1)S(1)} %all-to-all-done.2), channel_id=1, source_target_pairs={{0,1},{1,0},{2,3},{3,2},{4,5},{5,4},{6,7},{7,6},{8,9},{9,8},{10,11... | collective-permute-start | bytes 2752520 | tf_op jit(solution)/shard_map/ppermute | solution.py:12
  189.6 1.2 copy-start.1
